TPU v7x, 32 devices: a whole 2x2x4 slice. The times are simulated.
32 devices in a mesh: member: 4 (over y, core), lat: 8 (over z, x).
Axes of the slice: x: 2, y: 2, z: 4, core: 2. Of those that a mesh axis runs over, the one named last changes fastest.
Arguments:
- ensemble: float32 [640, 32, 256], P('member', 'lat'), may hold values from -6 to 6
- obs_cell: int32 [32, 128], P(('member', 'lat')), may hold values from 0 to 255
- obs_value: float32 [32, 128], P(('member', 'lat')), may hold values from -8 to 8
- obs_var: float32 [32, 128], P(('member', 'lat')), may hold values from 0.5 to 8
- patch_rows: int32 [32, 2], P(('member', 'lat')), may hold values from 1 to 24, 32 in all within a row
Outputs:
- analysis: float32 [640, 32, 256], P('member', 'lat')
Inputs may be any that keep to these rules, and one draw needn't show every extreme that they name: `patch_rows`: each server's 2 patch lengths sum to 32.
All inputs are finite; a program needn't handle non-finite values. Where the computation divides by a largest or mean magnitude, that divisor is 1e-20 or more.
Results may differ from a plain program's by a relative error of at most 0.0003.
Values sent between devices are 32-bit elements; how exact they have to be, the bound alone decides.
A program may use at most 64 MiB of HBM per device.

v0:
```python
import jax
import jax.numpy as jnp
from jax import lax
from jax.sharding import PartitionSpec as P

STEPS = 4
lat_coeff = 0.4
lon_coeff = 0.05
advect_coeff = 0.1


def with_halo(value, sides, width, wrap):
    for axis, dim in sides:
        size, length = (lax.axis_size(axis), value.shape[dim])
        up = [(i, (i + 1) % size) for i in range(size if wrap else size - 1)]
        down = [(j, i) for i, j in up]
        last = lax.slice_in_dim(value, length - width, length, axis=dim)
        initial = lax.slice_in_dim(value, 0, width, axis=dim)
        before = lax.ppermute(last, axis, up)
        after = lax.ppermute(initial, axis, down)
        value = jnp.concatenate([before, value, after], axis=dim)
    return value


def advance(padded):
    centre = padded[:, 1:-1]
    northern = padded[:, :-2]
    southern = padded[:, 2:]
    eastern = jnp.roll(centre, -1, axis=2)
    western = jnp.roll(centre, 1, axis=2)
    return (
        centre
        + lat_coeff * (northern + southern - 2.0 * centre)
        + lon_coeff * (eastern + western - 2.0 * centre)
        - advect_coeff * centre * (eastern - western)
    )


def observe(states, cell_index, values):
    observed = jnp.take(states, cell_index, axis=1)
    obs_mean = jnp.mean(observed, axis=0)
    return (observed - obs_mean, values - obs_mean)


def localize(obs_rows, rel_cols, first_row, row_count, lat_scale, width_cols):
    lower = first_row.astype(jnp.float32)
    upper = lower + row_count.astype(jnp.float32) - 1.0
    lat_gap = jnp.maximum(jnp.maximum(lower - obs_rows, obs_rows - upper), 0.0) / lat_scale
    lon_gap = jnp.maximum(jnp.maximum(-rel_cols, rel_cols - (width_cols - 1.0)), 0.0) / width_cols
    return jnp.exp(-lat_gap * lat_gap - lon_gap * lon_gap)


def dot3(left, right):
    return jnp.matmul(left, right, precision=lax.Precision.HIGH, preferred_element_type=jnp.float32)


def analyse(states, spread, obs_meta, lengths, width_cols):
    members = states.shape[0]
    cell_total = states.shape[1]
    lat_total = cell_total // width_cols
    near = spread.shape[1]
    state_mean = jnp.mean(states, axis=0)
    anomaly = states - state_mean
    starts = jnp.cumsum(lengths) - lengths
    cell_rows = jnp.arange(cell_total, dtype=jnp.int32) // width_cols
    identity = jnp.eye(members, dtype=jnp.float32)
    products = dot3(spread.T, jnp.concatenate([spread, anomaly], axis=1))
    common, crossed = (products[:, :near], products[:, near:])
    innov = obs_meta[0]
    shrink = jnp.zeros((cell_total,), jnp.float32)
    shift = state_mean
    weights_all = jnp.zeros((near, cell_total), jnp.float32)
    for patch in range(lengths.shape[0]):
        weights = (
            localize(
                obs_meta[2],
                obs_meta[3],
                starts[patch],
                lengths[patch],
                lat_total / 4.0,
                float(width_cols),
            )
            / obs_meta[1]
        )
        scale = jnp.sqrt(weights)
        gram_matrix = (members - 1.0) * identity + jnp.dot(
            spread * weights, spread.T, preferred_element_type=jnp.float32
        )
        bound = jnp.max(jnp.sum(jnp.abs(gram_matrix), axis=1))
        alpha = (members - 1.0) / bound
        x = common * scale[:, None] * (scale / bound)[None, :]
        c0 = 2.25 + alpha * (-2.4375 + alpha * (1.6875 + alpha * (-0.5625 + alpha * 0.0625)))
        c1 = -2.4375 + alpha * (3.375 + alpha * (-1.6875 + alpha * 0.25))
        c2 = 1.6875 + alpha * (-1.6875 + alpha * 0.375)
        c3 = -0.5625 + alpha * 0.25
        c4 = 0.0625
        x2 = dot3(x, x)
        x34 = dot3(x2, jnp.concatenate([x, x2], axis=1))
        x3, x4 = (x34[:, :near], x34[:, near:])
        low = c2 * x + c3 * x2 + c4 * x3
        high = c1 * x + c2 * x2 + c3 * x3 + c4 * x4
        block = jnp.concatenate([crossed * scale[:, None], (scale * innov)[:, None]], axis=1)
        both = dot3(jnp.concatenate([low, high], axis=0), block)
        b1 = c1 * block + both[:near]
        b2 = c0 * block + both[near:]
        b3 = c0 * b2 + dot3(high, b2)
        mixed = alpha * c0 * b1 + b3
        got = 1.5 * b1 - 0.5 * (
            alpha * c0 * c0 * b1
            + c0 * mixed
            + dot3(high, mixed)
            + alpha * (c1 * b3 + dot3(low, b3))
        )
        base = c0 * (1.5 - 0.5 * alpha * c0 * c0)
        driven = base * block[:, -1] + jnp.sum(x * got[:, -1][None, :], axis=1)
        again = jnp.sum(x * driven[None, :], axis=1)
        mean_part = (
            jnp.sum(block[:, :-1] * (base * driven)[:, None] + got[:, :-1] * again[:, None], axis=0)
            / bound
        )
        cell_mask = (cell_rows >= starts[patch]) & (cell_rows < starts[patch] + lengths[patch])
        root_scale = jnp.sqrt((members - 1.0) / bound)
        shift = shift + jnp.where(cell_mask, mean_part, 0.0)
        shrink = jnp.where(cell_mask, root_scale * base, shrink)
        weights_all = jnp.where(
            cell_mask[None, :], got[:, :-1] * (scale * (root_scale / bound))[:, None], weights_all
        )
    return shift + shrink * anomaly + dot3(spread, weights_all)


def per_device(ensemble, obs_cell, obs_value, obs_var, patch_rows):
    fields = ensemble
    members_dev = fields.shape[0]
    lat_rows = fields.shape[1]
    lon_cells = fields.shape[2]
    lat_count = lax.axis_size("lat")
    member_count = lax.axis_size("member")
    servers = lat_count * member_count
    width_cols = lon_cells // servers
    padded = with_halo(fields, (("lat", 1),), STEPS, False)
    global_rows = (
        lax.axis_index("lat") * lat_rows + jnp.arange(lat_rows + 2 * STEPS, dtype=jnp.int32) - STEPS
    )
    inside = ((global_rows >= 0) & (global_rows < lat_rows * lat_count)).astype(jnp.float32)
    for step_index in range(STEPS):
        padded = advance(padded)
        keeper = inside[step_index + 1 : inside.shape[0] - step_index - 1]
        padded = padded * keeper[None, :, None]
    fields = padded
    blocks = fields.reshape(1, members_dev, lat_rows, lon_cells)
    received = lax.all_to_all(blocks, ("member", "lat"), split_axis=3, concat_axis=0, tiled=True)
    strip = received.reshape(member_count, lat_count, members_dev, lat_rows, width_cols)
    strip = strip.transpose(0, 2, 1, 3, 4).reshape(
        member_count * members_dev, lat_count * lat_rows, width_cols
    )
    members = strip.shape[0]
    lat_total = strip.shape[1]
    states = strip.reshape(members, lat_total * width_cols)
    cell_index = obs_cell[0]
    obs_count = cell_index.shape[0]
    spread, innov = observe(states, cell_index, obs_value[0])
    obs_meta = jnp.stack(
        [
            innov,
            obs_var[0],
            (cell_index // width_cols).astype(jnp.float32),
            (cell_index % width_cols).astype(jnp.float32),
        ]
    )
    near_spread, near_meta = (
        with_halo(spread, ((("member", "lat"), 1),), obs_count, True),
        with_halo(obs_meta, ((("member", "lat"), 1),), obs_count, True),
    )
    shifts = jnp.repeat(jnp.array([-1.0, 0.0, 1.0], jnp.float32), obs_count) * width_cols
    near_meta = jnp.concatenate([near_meta[:3], (near_meta[3] + shifts)[None, :]], axis=0)
    analysed = analyse(states, near_spread, near_meta, patch_rows[0], width_cols)
    analysed = analysed.reshape(members, lat_total, width_cols)
    outgoing = analysed.reshape(member_count, members_dev, lat_count, lat_rows, width_cols)
    outgoing = outgoing.transpose(0, 2, 1, 3, 4).reshape(servers, members_dev, lat_rows, width_cols)
    returned = lax.all_to_all(outgoing, ("member", "lat"), split_axis=0, concat_axis=3, tiled=True)
    return returned.reshape(members_dev, lat_rows, lon_cells)


def solution(mesh):
    in_specs = (
        P("member", "lat", None),
        P(("member", "lat"), None),
        P(("member", "lat"), None),
        P(("member", "lat"), None),
        P(("member", "lat"), None),
    )
    out_specs = P("member", "lat", None)
    return jax.shard_map(
        per_device, mesh=mesh, in_specs=in_specs, out_specs=out_specs, check_vma=False
    )
```

profile of v0, /device:TPU:0, one launch (start us, length us, event | category | flops | bytes accessed | tf_op | source)
XLA Modules:
  0.0 164.4 jit_solution(16774635268156717155)
XLA Ops:
  0.0 1.3 copy.83
  1.3 4.9 %collective-permute-start = (f32[160,4,256]{2,0,1:T(8,128)S(1)}, f32[160,4,256]{2,0,1:T(8,128)S(1)}, u32[]{:S(2)}, u32[]{:S(2)}) collective-permute-start(f32[160,4,256]{2,0,1:T(8,128)S(1)} %copy.83), channel_id=1, source_target_pairs={{0,1},{1,2},{2,3},{3,4},{4,5},{5,6},{6,7},{8,9},{9,10},{10,11},{11... | collective-permute-start | bytes 1966088 | tf_op jit(solution)/shard_map/ppermute | solution.py:19
  6.2 1.3 collective-permute-start.1
  7.8 0.8 reduce-window.9
  8.6 25.5 %collective-permute-done = f32[160,4,256]{2,0,1:T(8,128)S(1)} collective-permute-done((f32[160,4,256]{2,0,1:T(8,128)S(1)}, f32[160,4,256]{2,0,1:T(8,128)S(1)}, u32[]{:S(2)}, u32[]{:S(2)}) %collective-permute-start) | collective-permute-done | bytes 655392 | tf_op jit(solution)/shard_map/ppermute | solution.py:19
  35.3 1.1 fusion.9
  37.0 0.9 fusion.25
  40.1 1.3 copy.86
  41.4 6.6 %all-to-all-start = ((f32[1,160,4,256]{1,2,0,3:T(4,128)}), f32[1,160,4,256]{1,2,0,3:T(4,128)S(1)}, u32[]{:S(2)}, u32[]{:S(2)}) async-start(f32[1,160,4,256]{1,2,0,3:T(4,128)} %copy.86), calls=%async_computation | async-start | bytes 2097152 | tf_op jit(solution)/shard_map/all_to_all | solution.py:151
  54.3 21.2 %all-to-all-done = f32[1,160,4,256]{1,2,0,3:T(4,128)S(1)} async-done(((f32[1,160,4,256]{1,2,0,3:T(4,128)}), f32[1,160,4,256]{1,2,0,3:T(4,128)S(1)}, u32[]{:S(2)}, u32[]{:S(2)}) %all-to-all-start) | async-done | bytes 655392 | tf_op jit(solution)/shard_map/all_to_all | solution.py:151
  77.0 0.8 gather_fusion
  78.2 0.8 collective-permute-start.4
  79.0 4.6 %collective-permute-start.5 = (f32[4,128]{1,0:T(4,128)S(1)}, f32[4,128]{1,0:T(4,128)S(1)}, u32[]{:S(2)}, u32[]{:S(2)}) collective-permute-start(f32[4,128]{1,0:T(4,128)S(1)} %pad_maximum_fusion.22), channel_id=1, source_target_pairs={{1,0},{2,1},{3,2},{4,3},{5,4},{6,5},{7,6},{8,7},{9,8},{10,9},{11,1... | collective-permute-start | bytes 6152 | tf_op jit(solution)/shard_map/ppermute | solution.py:20
  83.7 5.3 %collective-permute-start.3 = (f32[640,128]{1,0:T(8,128)S(1)}, f32[640,128]{1,0:T(8,128)}, u32[]{:S(2)}, u32[]{:S(2)}) collective-permute-start(f32[640,128]{1,0:T(8,128)S(1)} %subtract_bitcast_fusion), channel_id=1, source_target_pairs={{1,0},{2,1},{3,2},{4,3},{5,4},{6,5},{7,6},{8,7},{9,8},{10,9},{11,1... | collective-permute-start | bytes 983048 | tf_op jit(solution)/shard_map/ppermute | solution.py:20
  90.4 6.6 %collective-permute-done.2 = f32[640,128]{1,0:T(8,128)S(1)} collective-permute-done((f32[640,128]{1,0:T(8,128)S(1)}, f32[640,128]{1,0:T(8,128)S(1)}, u32[]{:S(2)}, u32[]{:S(2)}) %collective-permute-start.2) | collective-permute-done | bytes 327712 | tf_op jit(solution)/shard_map/ppermute | solution.py:19
  97.0 2.5 %collective-permute-done.3 = f32[640,128]{1,0:T(8,128)} collective-permute-done((f32[640,128]{1,0:T(8,128)S(1)}, f32[640,128]{1,0:T(8,128)}, u32[]{:S(2)}, u32[]{:S(2)}) %collective-permute-start.3) | collective-permute-done | bytes 327712 | tf_op jit(solution)/shard_map/ppermute | solution.py:20
  99.5 1.8 %fusion.3 = f32[640]{0:T(1024)S(1)} fusion(f32[640,128]{1,0:T(8,128)} %collective-permute-done.3, f32[640,128]{1,0:T(8,128)S(1)} %subtract_bitcast_fusion, f32[640,128]{1,0:T(8,128)S(1)} %collective-permute-done.2, f32[384]{0:T(512)S(1)} %get-tuple-element.25), kind=kOutput, calls=%fused_computation.6 | convolution fusion | flops 317848960 | bytes 987136 | tf_op jit(solution)/shard_map/dot_general | solution.py:86
  102.7 1.8 %fusion.1 = f32[640]{0:T(1024)S(1)} fusion(f32[640,128]{1,0:T(8,128)} %collective-permute-done.3, f32[640,128]{1,0:T(8,128)S(1)} %subtract_bitcast_fusion, f32[640,128]{1,0:T(8,128)S(1)} %collective-permute-done.2, f32[384]{0:T(512)S(1)} %get-tuple-element.53), kind=kOutput, calls=%fused_computation.4 | convolution fusion | flops 317848960 | bytes 987136 | tf_op jit(solution)/shard_map/dot_general | solution.py:86
  109.3 2.6 %fusion.10 = f32[384,640]{1,0:T(8,128)S(1)} fusion(f32[640,256]{1,0:T(8,128)S(1)} %broadcast_subtract_fusion, f32[640,128]{1,0:T(8,128)} %collective-permute-done.3, f32[640,128]{1,0:T(8,128)S(1)} %subtract_bitcast_fusion, f32[640,128]{1,0:T(8,128)S(1)} %collective-permute-done.2), kind=kOutput, calls=%fused_computation.16 | convolution fusion | flops 945438720 | bytes 2621440 | tf_op jit(solution)/shard_map/dot_general | solution.py:54
  113.0 0.8 copy-done
  113.9 2.1 %fusion.34 = f32[384,768]{1,0:T(8,128)} fusion(f32[384,384]{1,0:T(8,128)S(1)} %fusion.136, f32[384,384]{1,0:T(8,128)S(1)} %get-tuple-element.47), kind=kOutput, calls=%fused_computation.51 | convolution fusion | flops 679772160 | bytes 2359296 | tf_op jit(solution)/shard_map/dot_general | solution.py:54
  116.7 1.1 fusion.42
  118.4 1.3 fusion.46
  119.6 0.8 convolution_add_fusion.3
  121.2 1.0 fusion.32
  122.1 0.8 copy-done.3
  123.2 1.5 fusion.38
  126.3 0.9 fusion.28
  128.4 2.4 %fusion.104 = (f32[256]{0:T(256)S(1)}, pred[256]{0:T(512)(128)(4,1)S(1)}, pred[256]{0:T(512)(128)(4,1)S(1)}) fusion(f32[256]{0:T(256)S(1)} %add_reduce_fusion, f32[256]{0:T(256)S(1)} %copy-done.17, f32[256]{0:T(256)S(1)} %add_reduce_fusion.1, f32[]{:T(128)} %reduce_max.19, f32[]{:T(128)} %reduce_max.18, s32[]{:T(128)S(6)} %add.404, s32[]{:T(128)} %bitcast.8, ...), kind=kLoop, calls=%fused_computation.203 | loop fusion | flops 5120 | bytes 4632 | tf_op jit(solution)/shard_map/add | solution.py:123
  130.9 1.8 %convolution_add_fusion = f32[640,256]{1,0:T(8,128)S(1)} fusion(f32[640,256]{1,0:T(8,128)S(1)} %copy-done.7, f32[640,128]{1,0:T(8,128)} %collective-permute-done.3, f32[640,128]{1,0:T(8,128)S(1)} %copy-done.9, f32[640,128]{1,0:T(8,128)S(1)} %copy-done.11, f32[384,257]{1,0:T(8,128)S(1)} %copy-done.4, f32[384,257]{1,0:T(8,128)S(1)} %fusion.28, ...), kind=kOutput, calls=%fused_computation.36 | convolution fusion | flops 378863616 | bytes 3087360 | tf_op jit(solution)/shard_map/dot_general | solution.py:54
  133.9 29.2 %all_to_all.30 = f32[32,160,4,8]{1,3,2,0:T(8,128)S(1)} all-to-all(f32[32,160,4,8]{1,3,2,0:T(8,128)S(1)} %bitcast.110), channel_id=1, replica_groups=mesh['member'=4,'lat'=8] {'member','lat'}, dimensions={0} | all-to-all | bytes 1310720 | tf_op jit(solution)/shard_map/all_to_all | solution.py:180
  163.2 1.1 copy.107
  (128 shorter events, 19.1 us)
Async XLA Ops:
  0.0 34.2 %copy-start.5 = (f32[160,4,256]{2,1,0:T(4,128)S(1)}, f32[160,4,256]{2,1,0:T(4,128)}, u32[]{:S(2)}) copy-start(f32[160,4,256]{2,1,0:T(4,128)} %param.6) | copy-start | bytes 1966084
  1.3 32.9 %collective-permute-start = (f32[160,4,256]{2,0,1:T(8,128)S(1)}, f32[160,4,256]{2,0,1:T(8,128)S(1)}, u32[]{:S(2)}, u32[]{:S(2)}) collective-permute-start(f32[160,4,256]{2,0,1:T(8,128)S(1)} %copy.83), channel_id=1, source_target_pairs={{0,1},{1,2},{2,3},{3,4},{4,5},{5,6},{6,7},{8,9},{9,10},{10,11},{11... | collective-permute-start | bytes 1966088 | tf_op jit(solution)/shard_map/ppermute | solution.py:19
  6.2 28.2 %collective-permute-start.1 = (f32[160,4,256]{2,0,1:T(8,128)S(1)}, f32[160,4,256]{2,0,1:T(8,128)S(1)}, u32[]{:S(2)}, u32[]{:S(2)}) collective-permute-start(f32[160,4,256]{2,0,1:T(8,128)S(1)} %copy.83), channel_id=1, source_target_pairs={{1,0},{2,1},{3,2},{4,3},{5,4},{6,5},{7,6},{9,8},{10,9},{11,10},{12... | collective-permute-start | bytes 1966088 | tf_op jit(solution)/shard_map/ppermute | solution.py:20
  40.0 8.0 %copy-start.21 = (s32[1,2]{1,0:T(1,128)S(1)}, s32[1,2]{1,0:T(1,128)}, u32[]{:S(2)}) copy-start(s32[1,2]{1,0:T(1,128)} %param.10) | copy-start | bytes 28
  40.0 14.1 %copy-start.23 = (s32[1,128]{1,0:T(1,128)S(1)}, s32[1,128]{1,0:T(1,128)}, u32[]{:S(2)}) copy-start(s32[1,128]{1,0:T(1,128)} %param.7) | copy-start | bytes 1540
  40.1 14.1 %copy-start.20 = (f32[3]{0:T(128)S(1)}, f32[3]{0:T(128)}, u32[]{:S(2)}) copy-start(f32[3]{0:T(128)} %constant.157) | copy-start | bytes 40
  41.4 34.1 %all-to-all-start = ((f32[1,160,4,256]{1,2,0,3:T(4,128)}), f32[1,160,4,256]{1,2,0,3:T(4,128)S(1)}, u32[]{:S(2)}, u32[]{:S(2)}) async-start(f32[1,160,4,256]{1,2,0,3:T(4,128)} %copy.86), calls=%async_computation | async-start | bytes 2097152 | tf_op jit(solution)/shard_map/all_to_all | solution.py:151
  77.0 1.1 copy-start.24
  77.0 1.1 copy-start.22
  78.2 11.6 %collective-permute-start.4 = (f32[4,128]{1,0:T(4,128)S(1)}, f32[4,128]{1,0:T(4,128)S(1)}, u32[]{:S(2)}, u32[]{:S(2)}) collective-permute-start(f32[4,128]{1,0:T(4,128)S(1)} %pad_maximum_fusion.22), channel_id=1, source_target_pairs={{0,1},{1,2},{2,3},{3,4},{4,5},{5,6},{6,7},{7,8},{8,9},{9,10},{10,1... | collective-permute-start | bytes 6152 | tf_op jit(solution)/shard_map/ppermute | solution.py:19
  79.0 10.7 %collective-permute-start.5 = (f32[4,128]{1,0:T(4,128)S(1)}, f32[4,128]{1,0:T(4,128)S(1)}, u32[]{:S(2)}, u32[]{:S(2)}) collective-permute-start(f32[4,128]{1,0:T(4,128)S(1)} %pad_maximum_fusion.22), channel_id=1, source_target_pairs={{1,0},{2,1},{3,2},{4,3},{5,4},{6,5},{7,6},{8,7},{9,8},{10,9},{11,1... | collective-permute-start | bytes 6152 | tf_op jit(solution)/shard_map/ppermute | solution.py:20
  83.6 25.7 %copy-start.8 = (f32[640,128]{1,0:T(8,128)}, f32[640,128]{1,0:T(8,128)S(1)}, u32[]{:S(2)}) copy-start(f32[640,128]{1,0:T(8,128)S(1)} %subtract_bitcast_fusion) | copy-start | bytes 983044
  83.6 13.4 %collective-permute-start.2 = (f32[640,128]{1,0:T(8,128)S(1)}, f32[640,128]{1,0:T(8,128)S(1)}, u32[]{:S(2)}, u32[]{:S(2)}) collective-permute-start(f32[640,128]{1,0:T(8,128)S(1)} %subtract_bitcast_fusion), channel_id=1, source_target_pairs={{0,1},{1,2},{2,3},{3,4},{4,5},{5,6},{6,7},{7,8},{8,9},{9,10},{10,1... | collective-permute-start | bytes 983048 | tf_op jit(solution)/shard_map/ppermute | solution.py:19
  83.7 15.8 %collective-permute-start.3 = (f32[640,128]{1,0:T(8,128)S(1)}, f32[640,128]{1,0:T(8,128)}, u32[]{:S(2)}, u32[]{:S(2)}) collective-permute-start(f32[640,128]{1,0:T(8,128)S(1)} %subtract_bitcast_fusion), channel_id=1, source_target_pairs={{1,0},{2,1},{3,2},{4,3},{5,4},{6,5},{7,6},{8,7},{9,8},{10,9},{11,1... | collective-permute-start | bytes 983048 | tf_op jit(solution)/shard_map/ppermute | solution.py:20
  89.6 0.6 copy-start.16
  89.7 19.6 %copy-start.6 = (f32[640,256]{1,0:T(8,128)}, f32[640,256]{1,0:T(8,128)S(1)}, u32[]{:S(2)}) copy-start(f32[640,256]{1,0:T(8,128)S(1)} %broadcast_subtract_fusion) | copy-start | bytes 1966084
  89.8 18.1 %copy-start.12 = (f32[1,384]{1,0:T(1,128)}, f32[1,384]{1,0:T(1,128)S(1)}, u32[]{:S(2)}) copy-start(f32[1,384]{1,0:T(1,128)S(1)} %get-tuple-element.54) | copy-start | bytes 4612
  90.4 16.8 %copy-start.14 = (f32[1,384]{1,0:T(1,128)}, f32[1,384]{1,0:T(1,128)S(1)}, u32[]{:S(2)}) copy-start(f32[1,384]{1,0:T(1,128)S(1)} %get-tuple-element.26) | copy-start | bytes 4612
  97.0 12.3 %copy-start.10 = (f32[640,128]{1,0:T(8,128)}, f32[640,128]{1,0:T(8,128)S(1)}, u32[]{:S(2)}) copy-start(f32[640,128]{1,0:T(8,128)S(1)} %collective-permute-done.2) | copy-start | bytes 983044
  113.0 0.8 copy-start
  116.0 1.9 %copy-start.1 = (f32[384,384]{1,0:T(8,128)S(1)}, f32[384,384]{1,0:T(8,128)}, u32[]{:S(2)}) copy-start(f32[384,384]{1,0:T(8,128)} %copy-done) | copy-start | bytes 1769476
  116.0 1.9 %copy-start.2 = (f32[384,768]{1,0:T(8,128)S(1)}, f32[384,768]{1,0:T(8,128)}, u32[]{:S(2)}) copy-start(f32[384,768]{1,0:T(8,128)} %fusion.34) | copy-start | bytes 3538948
  122.1 0.8 copy-start.3
  126.2 1.3 copy-start.13
  126.2 1.3 copy-start.15
  127.2 1.1 copy-start.4
  127.3 1.1 copy-start.17
  127.4 3.5 %copy-start.7 = (f32[640,256]{1,0:T(8,128)S(1)}, f32[640,256]{1,0:T(8,128)}, u32[]{:S(2)}) copy-start(f32[640,256]{1,0:T(8,128)} %copy-done.6) | copy-start | bytes 1966084
  127.4 3.5 %copy-start.9 = (f32[640,128]{1,0:T(8,128)S(1)}, f32[640,128]{1,0:T(8,128)}, u32[]{:S(2)}) copy-start(f32[640,128]{1,0:T(8,128)} %copy-done.8) | copy-start | bytes 983044
  127.4 3.5 %copy-start.11 = (f32[640,128]{1,0:T(8,128)S(1)}, f32[640,128]{1,0:T(8,128)}, u32[]{:S(2)}) copy-start(f32[640,128]{1,0:T(8,128)} %copy-done.10) | copy-start | bytes 983044
  127.4 3.5 %copy-start.18 = (f32[384]{0:T(512)S(1)}, f32[384]{0:T(512)}, u32[]{:S(2)}) copy-start(f32[384]{0:T(512)} %get-tuple-element.12) | copy-start | bytes 4612
  127.4 3.5 %copy-start.19 = (f32[384]{0:T(512)S(1)}, f32[384]{0:T(512)}, u32[]{:S(2)}) copy-start(f32[384]{0:T(512)} %get-tuple-element.56) | copy-start | bytes 4612
where the time goes:
time: 165 us; the launch traced here: 164 us
  waiting for transfers between devices  55.9 us (34%)
  blocking collectives  29.2 us (18%)
  starting transfers between devices  23.6 us (14%)
  matrix products  20.3 us (12%)
  local copies, waits for them, and re-layouts  14.7 us (9%)
  other arithmetic  12.1 us (7%)
  between operations  8.58 us (5%)
    ppermute x3, waiting for transfers between devices, with_halo(): before = lax.ppermute(last, axis, up)  32.1 us
    all_to_all x1, blocking collectives, per_device(): lax.all_to_all(outgoing, ('member', 'lat'), split_axis=0, concat_axis=3,...  29.2 us
    all_to_all x1, waiting for transfers between devices, per_device(): lax.all_to_all(blocks, ('member', 'lat'), split_axis=3, concat_axis=0, ti...  21.2 us
    dot_general x14, matrix products, dot3(): jnp.matmul(left, right, precision=lax.Precision.HIGH, preferred_element_t...  16.7 us
    ppermute x3, starting transfers between devices, with_halo(): after = lax.ppermute(initial, axis, down)  11.2 us
    all_to_all x1, starting transfers between devices, per_device(): lax.all_to_all(blocks, ('member', 'lat'), split_axis=3, concat_axis=0, ti...  6.62 us
    ppermute x3, starting transfers between devices, with_halo(): before = lax.ppermute(last, axis, up)  5.8 us
    unnamed x54, local copies, waits for them, and re-layouts  3.6 us
  transfers between devices with their start and end apart: 7, of which 4 were waited for; matrix products, arithmetic and copies ran while one was open for 2% of the time, Pallas kernels for 0%

commit v1 on v0

--- a/solution.py
+++ b/solution.py
@@ -148,7 +148,15 @@
         padded = padded * keeper[None, :, None]
     fields = padded
     blocks = fields.reshape(1, members_dev, lat_rows, lon_cells)
-    received = lax.all_to_all(blocks, ("member", "lat"), split_axis=3, concat_axis=0, tiled=True)
+    received = jnp.concatenate(
+        lax.all_to_all(
+            jnp.stack(jnp.split(blocks, lax.axis_size(("member", "lat")), axis=3)),
+            ("member", "lat"),
+            0,
+            0,
+        ),
+        axis=0,
+    )
     strip = received.reshape(member_count, lat_count, members_dev, lat_rows, width_cols)
     strip = strip.transpose(0, 2, 1, 3, 4).reshape(
         member_count * members_dev, lat_count * lat_rows, width_cols

time: 165 us -> 221 us (1.34)
  local copies, waits for them, and re-layouts: 14.7 us -> 73.7 us
  matrix products: 20.3 us -> 16.1 us
    another operation x0 -> x36, local copies, waits for them, and re-layouts: none -> 42.7 us  [the longest x35 42 us: per_device(): jnp.stack(jnp.split(blocks, lax.axis_size(('member', 'lat')), axis=3))]
    unnamed x54 -> x119, local copies, waits for them, and re-layouts: 3.6 us -> 22.3 us
where the time goes in v1:
time: 221 us; the launch traced here: 219 us
  local copies, waits for them, and re-layouts  73.7 us (33%)
  waiting for transfers between devices  54.8 us (25%)
  blocking collectives  29.2 us (13%)
  starting transfers between devices  23.8 us (11%)
  matrix products  16.1 us (7%)
  other arithmetic  13 us (6%)
  between operations  8.67 us (4%)
    another operation x35, local copies, waits for them, and re-layouts, per_device(): jnp.stack(jnp.split(blocks, lax.axis_size(('member', 'lat')), axis=3))  42 us
    ppermute x3, waiting for transfers between devices, with_halo(): before = lax.ppermute(last, axis, up)  31.5 us
    all_to_all x1, blocking collectives, per_device(): lax.all_to_all(outgoing, ('member', 'lat'), split_axis=0, concat_axis=3,...  29.2 us
    unnamed x119, local copies, waits for them, and re-layouts  22.3 us
    all_to_all x1, waiting for transfers between devices, per_device(): lax.all_to_all(jnp.stack(jnp.split(blocks, lax.axis_size(('member', 'lat'...  21 us
    dot_general x14, matrix products, dot3(): jnp.matmul(left, right, precision=lax.Precision.HIGH, preferred_element_t...  14.7 us
    ppermute x3, starting transfers between devices, with_halo(): after = lax.ppermute(initial, axis, down)  11.2 us
    all_to_all x1, starting transfers between devices, per_device(): lax.all_to_all(jnp.stack(jnp.split(blocks, lax.axis_size(('member', 'lat'...  6.8 us
  transfers between devices with their start and end apart: 7, of which 4 were waited for; matrix products, arithmetic and copies ran while one was open for 2% of the time, Pallas kernels for 0%

profile of v1, /device:TPU:0, one launch (start us, length us, event | category | flops | bytes accessed | tf_op | source)
XLA Modules:
  0.0 219.3 jit_solution(9949395641370279676)
XLA Ops:
  0.0 1.3 copy.139
  1.3 4.9 %collective-permute-start = (f32[160,4,256]{2,0,1:T(8,128)S(1)}, f32[160,4,256]{2,0,1:T(8,128)S(1)}, u32[]{:S(2)}, u32[]{:S(2)}) collective-permute-start(f32[160,4,256]{2,0,1:T(8,128)S(1)} %copy.139), channel_id=1, source_target_pairs={{0,1},{1,2},{2,3},{3,4},{4,5},{5,6},{6,7},{8,9},{9,10},{10,11},{11... | collective-permute-start | bytes 1966088 | tf_op jit(solution)/shard_map/ppermute | solution.py:19
  6.2 1.3 collective-permute-start.1
  8.6 25.5 %collective-permute-done = f32[160,4,256]{2,0,1:T(8,128)S(1)} collective-permute-done((f32[160,4,256]{2,0,1:T(8,128)S(1)}, f32[160,4,256]{2,0,1:T(8,128)S(1)}, u32[]{:S(2)}, u32[]{:S(2)}) %collective-permute-start) | collective-permute-done | bytes 655392 | tf_op jit(solution)/shard_map/ppermute | solution.py:19
  40.0 3.1 %slice_bitcast_fusion.19 = (f32[1,1,160,4,8]{4,2,3,1,0:T(8,128)}, f32[1,1,160,4,8]{4,2,3,1,0:T(8,128)}, f32[1,1,160,4,8]{4,2,3,1,0:T(8,128)}, f32[1,1,160,4,8]{4...) fusion(f32[1,160,4,256]{3,1,2,0:T(8,128)S(1)} %fusion.62), kind=kLoop, calls=%fused_computation.146 | loop fusion | bytes 532480 | tf_op jit(solution)/shard_map/stack | solution.py:153
  43.1 3.1 %slice_bitcast_fusion = (f32[1,1,160,4,8]{4,2,3,1,0:T(8,128)S(1)}, f32[1,1,160,4,8]{4,2,3,1,0:T(8,128)S(1)}, f32[1,1,160,4,8]{4,2,3,1,0:T(8,128)S(1)}, f32[1,1,1...) fusion(f32[1,160,4,256]{3,1,2,0:T(8,128)S(1)} %fusion.62), kind=kLoop, calls=%fused_computation.127 | loop fusion | bytes 778240 | tf_op jit(solution)/shard_map/stack | solution.py:153
  48.0 1.7 copy.143
  49.7 1.7 copy.144
  51.5 1.7 copy.145
  53.2 1.7 copy.146
  55.0 1.7 copy.147
  56.7 1.7 copy.148
  58.4 1.8 copy.149
  60.2 1.7 copy.150
  61.9 1.7 copy.151
  63.7 1.7 copy.152
  65.4 1.7 copy.153
  67.2 1.7 copy.154
  68.9 1.8 copy.155
  70.7 1.7 copy.156
  101.0 6.8 %all-to-all-start = ((f32[32,1,160,4,8]{2,4,3,1,0:T(8,128)}), f32[32,1,160,4,8]{2,4,3,1,0:T(8,128)S(1)}, u32[]{:S(2)}, u32[]{:S(2)}) async-start(f32[32,1,160,4,8]{2,4,3,1,0:T(8,128)} %constant_dynamic-update-slice_fusion.3), calls=%async_computation | async-start | bytes 2097152 | tf_op jit(solution)/shard_map/all_to_all | solution.py:152
  114.0 21.0 %all-to-all-done = f32[32,1,160,4,8]{2,4,3,1,0:T(8,128)S(1)} async-done(((f32[32,1,160,4,8]{2,4,3,1,0:T(8,128)}), f32[32,1,160,4,8]{2,4,3,1,0:T(8,128)S(1)}, u32[]{:S(2)}, u32[]{:S(2)}) %all-to-all-start) | async-done | bytes 655392 | tf_op jit(solution)/shard_map/all_to_all | solution.py:152
  138.4 4.6 %collective-permute-start.5 = (f32[4,128]{1,0:T(4,128)S(1)}, f32[4,128]{1,0:T(4,128)S(1)}, u32[]{:S(2)}, u32[]{:S(2)}) collective-permute-start(f32[4,128]{1,0:T(4,128)S(1)} %pad_maximum_fusion.22), channel_id=1, source_target_pairs={{1,0},{2,1},{3,2},{4,3},{5,4},{6,5},{7,6},{8,7},{9,8},{10,9},{11,1... | collective-permute-start | bytes 6152 | tf_op jit(solution)/shard_map/ppermute | solution.py:20
  143.0 5.3 %collective-permute-start.3 = (f32[640,128]{1,0:T(8,128)S(1)}, f32[640,128]{1,0:T(8,128)S(1)}, u32[]{:S(2)}, u32[]{:S(2)}) collective-permute-start(f32[640,128]{1,0:T(8,128)S(1)} %subtract_bitcast_fusion), channel_id=1, source_target_pairs={{1,0},{2,1},{3,2},{4,3},{5,4},{6,5},{7,6},{8,7},{9,8},{10,9},{11,1... | collective-permute-start | bytes 983048 | tf_op jit(solution)/shard_map/ppermute | solution.py:20
  150.4 5.9 %collective-permute-done.2 = f32[640,128]{1,0:T(8,128)S(1)} collective-permute-done((f32[640,128]{1,0:T(8,128)S(1)}, f32[640,128]{1,0:T(8,128)S(1)}, u32[]{:S(2)}, u32[]{:S(2)}) %collective-permute-start.2) | collective-permute-done | bytes 327712 | tf_op jit(solution)/shard_map/ppermute | solution.py:19
  156.3 2.3 %collective-permute-done.3 = f32[640,128]{1,0:T(8,128)S(1)} collective-permute-done((f32[640,128]{1,0:T(8,128)S(1)}, f32[640,128]{1,0:T(8,128)S(1)}, u32[]{:S(2)}, u32[]{:S(2)}) %collective-permute-start.3) | collective-permute-done | bytes 327712 | tf_op jit(solution)/shard_map/ppermute | solution.py:20
  166.3 1.6 fusion.10
  169.8 2.1 fusion.34
  174.3 1.3 fusion.46
  179.4 1.3 fusion.38
  184.4 2.4 %fusion.104 = (f32[256]{0:T(256)S(1)}, pred[256]{0:T(512)(128)(4,1)S(1)}, pred[256]{0:T(512)(128)(4,1)S(1)}) fusion(f32[256]{0:T(256)S(1)} %add_reduce_fusion, f32[256]{0:T(256)S(1)} %copy-done.33, f32[256]{0:T(256)S(1)} %add_reduce_fusion.1, f32[]{:T(128)} %reduce_max.19, f32[]{:T(128)} %reduce_max.18, s32[]{:T(128)S(6)} %add.404, s32[]{:T(128)} %bitcast.38, ...), kind=kLoop, calls=%fused_computation.268 | loop fusion | flops 5120 | bytes 4632 | tf_op jit(solution)/shard_map/add | solution.py:123
  188.9 29.2 %all_to_all.20 = f32[32,160,4,8]{1,3,2,0:T(8,128)S(1)} all-to-all(f32[32,160,4,8]{1,3,2,0:T(8,128)S(1)} %bitcast.169), channel_id=1, replica_groups=mesh['member'=4,'lat'=8] {'member','lat'}, dimensions={0} | all-to-all | bytes 1310720 | tf_op jit(solution)/shard_map/all_to_all | solution.py:188
  (225 shorter events, 63.2 us)
Async XLA Ops:
  0.0 34.2 %copy-start.5 = (f32[160,4,256]{2,1,0:T(4,128)S(1)}, f32[160,4,256]{2,1,0:T(4,128)}, u32[]{:S(2)}) copy-start(f32[160,4,256]{2,1,0:T(4,128)} %param.6) | copy-start | bytes 1966084
  1.3 32.9 %collective-permute-start = (f32[160,4,256]{2,0,1:T(8,128)S(1)}, f32[160,4,256]{2,0,1:T(8,128)S(1)}, u32[]{:S(2)}, u32[]{:S(2)}) collective-permute-start(f32[160,4,256]{2,0,1:T(8,128)S(1)} %copy.139), channel_id=1, source_target_pairs={{0,1},{1,2},{2,3},{3,4},{4,5},{5,6},{6,7},{8,9},{9,10},{10,11},{11... | collective-permute-start | bytes 1966088 | tf_op jit(solution)/shard_map/ppermute | solution.py:19
  6.2 28.2 %collective-permute-start.1 = (f32[160,4,256]{2,0,1:T(8,128)S(1)}, f32[160,4,256]{2,0,1:T(8,128)S(1)}, u32[]{:S(2)}, u32[]{:S(2)}) collective-permute-start(f32[160,4,256]{2,0,1:T(8,128)S(1)} %copy.139), channel_id=1, source_target_pairs={{1,0},{2,1},{3,2},{4,3},{5,4},{6,5},{7,6},{9,8},{10,9},{11,10},{12... | collective-permute-start | bytes 1966088 | tf_op jit(solution)/shard_map/ppermute | solution.py:20
  80.7 3.9 %copy-start.23 = (f32[1,1,160,4,8]{2,4,3,1,0:T(8,128)S(1)}, f32[1,1,160,4,8]{2,4,3,1,0:T(8,128)}, u32[]{:S(2)}) copy-start(f32[1,1,160,4,8]{2,4,3,1,0:T(8,128)} %copy.147) | copy-start | bytes 61444
  80.7 4.5 %copy-start.22 = (f32[1,1,160,4,8]{2,4,3,1,0:T(8,128)S(1)}, f32[1,1,160,4,8]{2,4,3,1,0:T(8,128)}, u32[]{:S(2)}) copy-start(f32[1,1,160,4,8]{2,4,3,1,0:T(8,128)} %copy.148) | copy-start | bytes 61444
  80.7 5.1 %copy-start.21 = (f32[1,1,160,4,8]{2,4,3,1,0:T(8,128)S(1)}, f32[1,1,160,4,8]{2,4,3,1,0:T(8,128)}, u32[]{:S(2)}) copy-start(f32[1,1,160,4,8]{2,4,3,1,0:T(8,128)} %copy.149) | copy-start | bytes 61444
  80.7 5.7 %copy-start.20 = (f32[1,1,160,4,8]{2,4,3,1,0:T(8,128)S(1)}, f32[1,1,160,4,8]{2,4,3,1,0:T(8,128)}, u32[]{:S(2)}) copy-start(f32[1,1,160,4,8]{2,4,3,1,0:T(8,128)} %copy.150) | copy-start | bytes 61444
  80.8 6.3 %copy-start.19 = (f32[1,1,160,4,8]{2,4,3,1,0:T(8,128)S(1)}, f32[1,1,160,4,8]{2,4,3,1,0:T(8,128)}, u32[]{:S(2)}) copy-start(f32[1,1,160,4,8]{2,4,3,1,0:T(8,128)} %copy.151) | copy-start | bytes 61444
  80.9 6.7 %copy-start.18 = (f32[1,1,160,4,8]{2,4,3,1,0:T(8,128)S(1)}, f32[1,1,160,4,8]{2,4,3,1,0:T(8,128)}, u32[]{:S(2)}) copy-start(f32[1,1,160,4,8]{2,4,3,1,0:T(8,128)} %copy.152) | copy-start | bytes 61444
  80.9 7.3 %copy-start.16 = (f32[1,1,160,4,8]{2,4,3,1,0:T(8,128)S(1)}, f32[1,1,160,4,8]{2,4,3,1,0:T(8,128)}, u32[]{:S(2)}) copy-start(f32[1,1,160,4,8]{2,4,3,1,0:T(8,128)} %copy.153) | copy-start | bytes 61444
  80.9 7.9 %copy-start.17 = (f32[1,1,160,4,8]{2,4,3,1,0:T(8,128)S(1)}, f32[1,1,160,4,8]{2,4,3,1,0:T(8,128)}, u32[]{:S(2)}) copy-start(f32[1,1,160,4,8]{2,4,3,1,0:T(8,128)} %copy.154) | copy-start | bytes 61444
  80.9 8.5 %copy-start.15 = (f32[1,1,160,4,8]{2,4,3,1,0:T(8,128)S(1)}, f32[1,1,160,4,8]{2,4,3,1,0:T(8,128)}, u32[]{:S(2)}) copy-start(f32[1,1,160,4,8]{2,4,3,1,0:T(8,128)} %copy.155) | copy-start | bytes 61444
  81.0 9.1 %copy-start.14 = (f32[1,1,160,4,8]{2,4,3,1,0:T(8,128)S(1)}, f32[1,1,160,4,8]{2,4,3,1,0:T(8,128)}, u32[]{:S(2)}) copy-start(f32[1,1,160,4,8]{2,4,3,1,0:T(8,128)} %copy.156) | copy-start | bytes 61444
  90.1 17.7 %copy-start.38 = (s32[1,2]{1,0:T(1,128)S(1)}, s32[1,2]{1,0:T(1,128)}, u32[]{:S(2)}) copy-start(s32[1,2]{1,0:T(1,128)} %param.10) | copy-start | bytes 28
  90.7 23.2 %copy-start.40 = (s32[1,128]{1,0:T(1,128)S(1)}, s32[1,128]{1,0:T(1,128)}, u32[]{:S(2)}) copy-start(s32[1,128]{1,0:T(1,128)} %param.7) | copy-start | bytes 1540
  90.7 23.3 %copy-start.36 = (f32[3]{0:T(128)S(1)}, f32[3]{0:T(128)}, u32[]{:S(2)}) copy-start(f32[3]{0:T(128)} %constant.157) | copy-start | bytes 40
  101.0 34.1 %all-to-all-start = ((f32[32,1,160,4,8]{2,4,3,1,0:T(8,128)}), f32[32,1,160,4,8]{2,4,3,1,0:T(8,128)S(1)}, u32[]{:S(2)}, u32[]{:S(2)}) async-start(f32[32,1,160,4,8]{2,4,3,1,0:T(8,128)} %constant_dynamic-update-slice_fusion.3), calls=%async_computation | async-start | bytes 2097152 | tf_op jit(solution)/shard_map/all_to_all | solution.py:152
  137.5 12.4 %collective-permute-start.4 = (f32[4,128]{1,0:T(4,128)S(1)}, f32[4,128]{1,0:T(4,128)S(1)}, u32[]{:S(2)}, u32[]{:S(2)}) collective-permute-start(f32[4,128]{1,0:T(4,128)S(1)} %pad_maximum_fusion.22), channel_id=1, source_target_pairs={{0,1},{1,2},{2,3},{3,4},{4,5},{5,6},{6,7},{7,8},{8,9},{9,10},{10,1... | collective-permute-start | bytes 6152 | tf_op jit(solution)/shard_map/ppermute | solution.py:19
  138.4 11.6 %collective-permute-start.5 = (f32[4,128]{1,0:T(4,128)S(1)}, f32[4,128]{1,0:T(4,128)S(1)}, u32[]{:S(2)}, u32[]{:S(2)}) collective-permute-start(f32[4,128]{1,0:T(4,128)S(1)} %pad_maximum_fusion.22), channel_id=1, source_target_pairs={{1,0},{2,1},{3,2},{4,3},{5,4},{6,5},{7,6},{8,7},{9,8},{10,9},{11,1... | collective-permute-start | bytes 6152 | tf_op jit(solution)/shard_map/ppermute | solution.py:20
  143.0 23.3 %copy-start.8 = (f32[640,128]{1,0:T(8,128)}, f32[640,128]{1,0:T(8,128)S(1)}, u32[]{:S(2)}) copy-start(f32[640,128]{1,0:T(8,128)S(1)} %subtract_bitcast_fusion) | copy-start | bytes 983044
  143.0 13.4 %collective-permute-start.2 = (f32[640,128]{1,0:T(8,128)S(1)}, f32[640,128]{1,0:T(8,128)S(1)}, u32[]{:S(2)}, u32[]{:S(2)}) collective-permute-start(f32[640,128]{1,0:T(8,128)S(1)} %subtract_bitcast_fusion), channel_id=1, source_target_pairs={{0,1},{1,2},{2,3},{3,4},{4,5},{5,6},{6,7},{7,8},{8,9},{9,10},{10,1... | collective-permute-start | bytes 983048 | tf_op jit(solution)/shard_map/ppermute | solution.py:19
  143.0 15.6 %collective-permute-start.3 = (f32[640,128]{1,0:T(8,128)S(1)}, f32[640,128]{1,0:T(8,128)S(1)}, u32[]{:S(2)}, u32[]{:S(2)}) collective-permute-start(f32[640,128]{1,0:T(8,128)S(1)} %subtract_bitcast_fusion), channel_id=1, source_target_pairs={{1,0},{2,1},{3,2},{4,3},{5,4},{6,5},{7,6},{8,7},{9,8},{10,9},{11,1... | collective-permute-start | bytes 983048 | tf_op jit(solution)/shard_map/ppermute | solution.py:20
  149.8 9.5 %copy-start.32 = (f32[256]{0:T(256)}, f32[256]{0:T(256)S(1)}, u32[]{:S(2)}) copy-start(f32[256]{0:T(256)S(1)} %div.166) | copy-start | bytes 3076
  149.9 16.4 %copy-start.6 = (f32[640,256]{1,0:T(8,128)}, f32[640,256]{1,0:T(8,128)S(1)}, u32[]{:S(2)}) copy-start(f32[640,256]{1,0:T(8,128)S(1)} %broadcast_subtract_fusion) | copy-start | bytes 1966084
  150.0 14.9 %copy-start.28 = (f32[1,384]{1,0:T(1,128)}, f32[1,384]{1,0:T(1,128)S(1)}, u32[]{:S(2)}) copy-start(f32[1,384]{1,0:T(1,128)S(1)} %get-tuple-element.84) | copy-start | bytes 4612
  150.4 13.8 %copy-start.30 = (f32[1,384]{1,0:T(1,128)}, f32[1,384]{1,0:T(1,128)S(1)}, u32[]{:S(2)}) copy-start(f32[1,384]{1,0:T(1,128)S(1)} %get-tuple-element.26) | copy-start | bytes 4612
  156.3 9.9 %copy-start.10 = (f32[640,128]{1,0:T(8,128)}, f32[640,128]{1,0:T(8,128)S(1)}, u32[]{:S(2)}) copy-start(f32[640,128]{1,0:T(8,128)S(1)} %collective-permute-done.2) | copy-start | bytes 983044
  158.6 7.7 %copy-start.12 = (f32[640,128]{1,0:T(8,128)}, f32[640,128]{1,0:T(8,128)S(1)}, u32[]{:S(2)}) copy-start(f32[640,128]{1,0:T(8,128)S(1)} %collective-permute-done.3) | copy-start | bytes 983044
  160.7 4.8 %copy-start.37 = (f32[3]{0:T(128)S(1)}, f32[3]{0:T(128)}, u32[]{:S(2)}) copy-start(f32[3]{0:T(128)} %constant.157) | copy-start | bytes 40
  183.3 3.5 %copy-start.7 = (f32[640,256]{1,0:T(8,128)S(1)}, f32[640,256]{1,0:T(8,128)}, u32[]{:S(2)}) copy-start(f32[640,256]{1,0:T(8,128)} %copy-done.6) | copy-start | bytes 1966084
  183.3 3.5 %copy-start.9 = (f32[640,128]{1,0:T(8,128)S(1)}, f32[640,128]{1,0:T(8,128)}, u32[]{:S(2)}) copy-start(f32[640,128]{1,0:T(8,128)} %copy-done.8) | copy-start | bytes 983044
  183.3 3.5 %copy-start.11 = (f32[640,128]{1,0:T(8,128)S(1)}, f32[640,128]{1,0:T(8,128)}, u32[]{:S(2)}) copy-start(f32[640,128]{1,0:T(8,128)} %copy-done.10) | copy-start | bytes 983044
  (17 other events, 33.1 us)
